TPU v7x, 32 devices: a whole 2x2x4 slice. The times are simulated.
32 devices in a mesh: grp: 4 (over y, core), rows: 8 (over z, x).
Axes of the slice: x: 2, y: 2, z: 4, core: 2. Of those that a mesh axis runs over, the one named last changes fastest.
Arguments:
- rhs: float32 [2048, 64, 128], P(('grp', 'rows')), may hold values from -6 to 6
- fine_diag: bfloat16 [2048, 64, 64], P(('grp', 'rows')), may hold values from -0.2 to 1.2
- fine_smoother: bfloat16 [2048, 64, 64], P(('grp', 'rows')), may hold values from -4 to 4
- fine_blocks: bfloat16 [2048, 7, 64, 64], P(('grp', 'rows')), may hold values from -0.1796875 to 0.1796875
- fine_cols: int32 [2048, 7], P(('grp', 'rows')), may hold values from 0 to 2047, as said below
- aggregate: int32 [2048], P(('grp', 'rows')), may hold values from 0 to 511, as said below
- coarse_diag: bfloat16 [512, 64, 64], P('rows'), may hold values from -0.8 to 4.8
- coarse_smoother: bfloat16 [512, 64, 64], P('rows'), may hold values from -1 to 1
- coarse_blocks: bfloat16 [512, 7, 64, 64], P('rows'), may hold values from -0.71875 to 0.71875
- coarse_cols: int32 [512, 7], P('rows'), may hold values from 0 to 511, as said below
Outputs:
- solution: float32 [2048, 64, 128], P(('grp', 'rows'))
Inputs may be any that keep to these rules, and one draw needn't show every extreme that they name: fine_cols row i names rows within 32 of i; the distance 32 is reached. coarse_cols row c names rows within 32 of c; the distance 32 is reached. `aggregate`: aggregate_i lies in [r * 64, (r + 1) * 64) with r = (i // 64) mod 8.
All inputs are finite; a program needn't handle non-finite values.
Results may differ from a plain program's by a relative error of at most 0.001.
The roundings to bfloat16 on the way count: a program that leaves them out, or rounds other values in their place, can miss the bound.
Values may be sent and summed in bfloat16 or wider, within the bound.
A program may use at most 128 MiB of HBM per device.

v0:
```python
import jax
import jax.numpy as jnp
from jax import lax
from jax.sharding import PartitionSpec as P

damping = 0.8


def extended_2(cells, sides, width):
    for axis, dim in sides:
        count = lax.axis_size(axis)
        ends = count - 1
        head = lax.slice_in_dim(cells, 0, width, axis=dim)
        tail = lax.slice_in_dim(cells, cells.shape[dim] - width, cells.shape[dim], axis=dim)
        cells = jnp.concatenate(
            [
                lax.ppermute(tail, axis, [(i, (i + 1) % count) for i in range(ends)]),
                cells,
                lax.ppermute(head, axis, [((i + 1) % count, i) for i in range(ends)]),
            ],
            axis=dim,
        )
    return cells


def block_product(blocks, vector):
    return jnp.einsum(
        "nab,nbk->nak", blocks, vector.astype(jnp.bfloat16), preferred_element_type=jnp.float32
    )


def nearby_product(off_blocks, columns, extended, first_row):
    nearby = jnp.take(extended, columns - first_row, axis=0)
    return jnp.einsum("njab,njbk->nak", off_blocks, nearby, preferred_element_type=jnp.float32)


def fine_operator(fine_diag, fine_blocks, fine_cols, vector):
    rounded_rows = vector.astype(jnp.bfloat16)
    height = vector.shape[0]
    margin = height // 2
    extended = extended_2(rounded_rows, ((("grp", "rows"), 0),), margin)
    first_row = lax.axis_index(("grp", "rows")) * height - margin
    return block_product(fine_diag, rounded_rows) + nearby_product(
        fine_blocks, fine_cols, extended, first_row
    )


def coarse_nearby(off_blocks, columns, rounded_full):
    height = rounded_full.shape[0]
    margin = height // 2
    extended = extended_2(rounded_full, (("rows", 0),), margin)
    first_row = lax.axis_index("rows") * height - margin
    return nearby_product(off_blocks, columns, extended, first_row)


def on_device(
    rhs,
    fine_diag,
    fine_smoother,
    fine_blocks,
    fine_cols,
    aggregate,
    coarse_diag,
    coarse_smoother,
    coarse_blocks,
    coarse_cols,
):
    first_iterate = damping * block_product(fine_smoother, rhs)
    first_residual = rhs - fine_operator(fine_diag, fine_blocks, fine_cols, first_iterate)
    second_iterate = first_iterate + damping * block_product(fine_smoother, first_residual)
    second_residual = rhs - fine_operator(fine_diag, fine_blocks, fine_cols, second_iterate)
    coarse_height = coarse_diag.shape[0]
    local_index = aggregate - lax.axis_index("rows") * coarse_height
    selector = (local_index[:, None] == jnp.arange(coarse_height, dtype=jnp.int32)[None, :]).astype(
        jnp.float32
    )
    partial_sum = jnp.einsum(
        "fc,fak->cak", selector, second_residual, precision=lax.Precision.HIGHEST
    )
    coarse_rhs = lax.psum(partial_sum, "grp")
    coarse_first = damping * block_product(coarse_smoother, coarse_rhs)
    rounded_first = coarse_first.astype(jnp.bfloat16)
    coarse_image = block_product(coarse_diag, rounded_first) + coarse_nearby(
        coarse_blocks, coarse_cols, rounded_first
    )
    coarse_second = coarse_first + damping * block_product(
        coarse_smoother, coarse_rhs - coarse_image
    )
    return second_iterate + jnp.take(coarse_second, local_index, axis=0)


def solution(mesh):
    in_specs = (
        P(("grp", "rows"), None, None),
        P(("grp", "rows"), None, None),
        P(("grp", "rows"), None, None),
        P(("grp", "rows"), None, None, None),
        P(("grp", "rows"), None),
        P(("grp", "rows")),
        P("rows", None, None),
        P("rows", None, None),
        P("rows", None, None, None),
        P("rows", None),
    )
    out_specs = P(("grp", "rows"), None, None)
    return jax.shard_map(
        on_device, mesh=mesh, in_specs=in_specs, out_specs=out_specs, check_vma=False
    )
```

profile of v0, /device:TPU:0, one launch (start us, length us, event | category | flops | bytes accessed | tf_op | source)
XLA Modules:
  0.0 246.3 jit_solution(17737860054501911996)
XLA Ops:
  7.8 3.4 %multiply_convert_fusion.1 = (bf16[64,64,128]{2,1,0:T(8,128)(2,1)S(1)}, f32[64,64,128]{2,1,0:T(8,128)}) fusion(bf16[64,64,64]{2,1,0:T(8,128)(2,1)S(1)} %copy-done, f32[64,64,128]{2,1,0:T(8,128)} %param.12), kind=kOutput, calls=%fused_computation.33 | convolution fusion | flops 68681728 | bytes 5767168 | tf_op jit(solution)/shard_map/nab,nbk->nak/dot_general | solution.py:27
  13.6 6.3 %collective-permute-start = (bf16[32,64,128]{2,1,0:T(8,128)(2,1)}, bf16[32,64,128]{2,1,0:T(8,128)(2,1)}, u32[]{:S(2)}, u32[]{:S(2)}) collective-permute-start(bf16[32,64,128]{2,1,0:T(8,128)(2,1)} %get-tuple-element.16), channel_id=1, source_target_pairs={{0,1},{1,2},{2,3},{3,4},{4,5},{5,6},{6,7},{7,8},{8,9},{9,10},{10,1... | collective-permute-start | bytes 1572872 | tf_op jit(solution)/shard_map/ppermute | solution.py:17
  20.3 1.8 fusion.43
  22.1 18.5 %collective-permute-done.1 = bf16[32,64,128]{2,1,0:T(8,128)(2,1)} collective-permute-done((bf16[32,64,128]{2,1,0:T(8,128)(2,1)}, bf16[32,64,128]{2,1,0:T(8,128)(2,1)}, u32[]{:S(2)}, u32[]{:S(2)}) %collective-permute-start.1) | collective-permute-done | bytes 524320 | tf_op jit(solution)/shard_map/ppermute | solution.py:19
  42.4 13.3 %gather_fusion.1 = bf16[448,64,128]{2,1,0:T(8,128)(2,1)} fusion(bf16[128,64,128]{2,1,0:T(8,128)(2,1)S(1)} %pad_maximum_fusion, s32[1024]{0:T(1024)S(1)} %pad_clamp_fusion.2), kind=kCustom, calls=%fused_computation.clone | custom fusion | bytes 14681856 | tf_op jit(solution)/shard_map/jit(_take)/gather | solution.py:33
  55.8 10.1 %fusion.40 = (bf16[64,64,128]{2,1,0:T(8,128)(2,1)S(1)}, f32[64,64,128]{2,1,0:T(8,128)}) fusion(bf16[64,64,64]{2,1,0:T(8,128)(2,1)S(1)} %copy-done, f32[64,64,128]{2,1,0:T(8,128)} %param.12, f32[64,128,64]{1,2,0:T(8,128)} %fusion.43, bf16[64,7,64,64]{3,2,1,0:T(8,128)(2,1)} %param.15, bf16[64,7,64,128]{3,2,1,0:T(8,128)(2,1)} %bitcast.56, ...), kind=kOutput, calls=%fused_computation.61 | convolution fusion | flops 544210944 | bytes 20971968 | tf_op jit(solution)/shard_map/nab,nbk->nak/dot_general | solution.py:27
  67.4 5.2 %collective-permute-start.2 = (bf16[32,64,128]{2,1,0:T(8,128)(2,1)S(1)}, bf16[32,64,128]{2,1,0:T(8,128)(2,1)S(1)}, u32[]{:S(2)}, u32[]{:S(2)}) collective-permute-start(bf16[32,64,128]{2,1,0:T(8,128)(2,1)S(1)} %get-tuple-element.14), channel_id=1, source_target_pairs={{0,1},{1,2},{2,3},{3,4},{4,5},{5,6},{6,7},{7,8},{8,9},{9,10},{10,1... | collective-permute-start | bytes 1572872 | tf_op jit(solution)/shard_map/ppermute | solution.py:17
  72.7 1.8 fusion.44
  74.5 19.4 %collective-permute-done.3 = bf16[32,64,128]{2,1,0:T(8,128)(2,1)S(1)} collective-permute-done((bf16[32,64,128]{2,1,0:T(8,128)(2,1)S(1)}, bf16[32,64,128]{2,1,0:T(8,128)(2,1)S(1)}, u32[]{:S(2)}, u32[]{:S(2)}) %collective-permute-start.3) | collective-permute-done | bytes 524320 | tf_op jit(solution)/shard_map/ppermute | solution.py:19
  95.5 13.3 %gather_fusion.2 = bf16[448,64,128]{2,1,0:T(8,128)(2,1)} fusion(bf16[128,64,128]{2,1,0:T(8,128)(2,1)S(1)} %pad_maximum_fusion.1, s32[1024]{0:T(1024)S(1)} %pad_clamp_fusion.2), kind=kCustom, calls=%fused_computation.1.clone | custom fusion | bytes 14681856 | tf_op jit(solution)/shard_map/jit(_take)/gather | solution.py:33
  108.9 9.2 %bitcast_subtract_fusion.1 = f32[64,64,128]{2,1,0:T(8,128)S(1)} fusion(f32[64,64,128]{2,1,0:T(8,128)} %param.12, f32[64,128,64]{1,2,0:T(8,128)} %fusion.44, bf16[64,7,64,64]{3,2,1,0:T(8,128)(2,1)} %param.15, bf16[64,7,64,128]{3,2,1,0:T(8,128)(2,1)} %bitcast.57, pred[64,7]{1,0:T(8,128)(4,1)S(1)} %copy.17), kind=kOutput, calls=%fused_computation.22 | convolution fusion | flops 474480640 | bytes 17301952 | tf_op jit(solution)/shard_map/njab,njbk->nak/dot_general | solution.py:34
  118.1 3.8 %fusion.14 = f32[64,64,128]{2,0,1:T(8,128)} fusion(f32[64,64,128]{2,1,0:T(8,128)S(1)} %bitcast_subtract_fusion.1, s32[64]{0:T(128)S(1)} %get-tuple-element.7), kind=kOutput, calls=%fused_computation.28 | convolution fusion | flops 402657280 | bytes 4194560 | tf_op jit(solution)/shard_map/fc,fak->cak/dot_general | solution.py:77
  122.8 51.9 %all-reduce.2.cloned.1.call-done = f32[64,64,128]{2,0,1:T(8,128)} async-done(((f32[64,64,128]{2,0,1:T(8,128)}), f32[64,64,128]{2,0,1:T(8,128)}) %all-reduce.2.cloned.1.call-update) | async-done | bytes 2097168 | tf_op jit(solution)/shard_map/psum | solution.py:80
  176.5 2.3 fusion.23
  182.0 5.3 %collective-permute-start.4 = (bf16[32,64,128]{2,1,0:T(8,128)(2,1)}, bf16[32,64,128]{2,1,0:T(8,128)(2,1)}, u32[]{:S(2)}, u32[]{:S(2)}) collective-permute-start(bf16[32,64,128]{2,1,0:T(8,128)(2,1)} %get-tuple-element.12), channel_id=1, source_target_pairs={{0,1},{1,2},{2,3},{3,4},{4,5},{5,6},{6,7},{8,9},{9,10},{10,11},{11... | collective-permute-start | bytes 1572872 | tf_op jit(solution)/shard_map/ppermute | solution.py:17
  187.5 3.1 %fusion.28 = f32[64,128,64]{1,2,0:T(8,128)} fusion(bf16[64,64,64]{2,1,0:T(8,128)(2,1)} %param.18, f32[64,128,64]{1,2,0:T(8,128)S(1)} %fusion.23), kind=kOutput, calls=%fused_computation.40 | convolution fusion | flops 68157440 | bytes 4718592 | tf_op jit(solution)/shard_map/nab,nbk->nak/dot_general | solution.py:27
  190.6 5.6 %collective-permute-done.5 = bf16[32,64,128]{2,1,0:T(8,128)(2,1)} collective-permute-done((bf16[32,64,128]{2,1,0:T(8,128)(2,1)}, bf16[32,64,128]{2,1,0:T(8,128)(2,1)}, u32[]{:S(2)}, u32[]{:S(2)}) %collective-permute-start.5) | collective-permute-done | bytes 524320 | tf_op jit(solution)/shard_map/ppermute | solution.py:19
  196.1 11.1 %collective-permute-done.4 = bf16[32,64,128]{2,1,0:T(8,128)(2,1)} collective-permute-done((bf16[32,64,128]{2,1,0:T(8,128)(2,1)}, bf16[32,64,128]{2,1,0:T(8,128)(2,1)}, u32[]{:S(2)}, u32[]{:S(2)}) %collective-permute-start.4) | collective-permute-done | bytes 524320 | tf_op jit(solution)/shard_map/ppermute | solution.py:17
  208.7 13.3 %gather_fusion.3 = bf16[448,64,128]{2,1,0:T(8,128)(2,1)} fusion(bf16[128,64,128]{2,1,0:T(8,128)(2,1)S(1)} %pad_maximum_fusion.2, s32[1024]{0:T(1024)S(1)} %pad_clamp_fusion.1), kind=kCustom, calls=%fused_computation.2.clone | custom fusion | bytes 14681856 | tf_op jit(solution)/shard_map/jit(_take)/gather | solution.py:33
  222.1 6.8 %fusion = f32[64,128,64,1]{1,2,3,0:T(8,128)S(1)} fusion(bf16[64,7,64,64]{3,2,1,0:T(8,128)(2,1)} %param.20, bf16[64,7,64,128]{3,2,1,0:T(8,128)(2,1)} %bitcast.58, pred[64,7]{1,0:T(8,128)(4,1)S(1)} %copy.23), kind=kOutput, calls=%fused_computation.4 | convolution fusion | flops 473432064 | bytes 13107648 | tf_op jit(solution)/shard_map/njab,njbk->nak/dot_general | solution.py:34
  228.9 2.4 fusion.12
  231.3 2.6 %add_bitcast_fusion = f32[64,64,128]{2,1,0:T(8,128)} fusion(f32[64,128,64]{1,2,0:T(8,128)S(1)} %copy-done.3, bf16[64,64,64]{2,1,0:T(8,128)(2,1)S(1)} %copy-done.10, bf16[64,64,128]{2,0,1:T(8,128)(2,1)S(1)} %fusion.12), kind=kOutput, calls=%fused_computation.31 | convolution fusion | flops 68681728 | bytes 5767168 | tf_op jit(solution)/shard_map/nab,nbk->nak/dot_general | solution.py:27
  233.9 2.3 gather_fusion
  236.2 3.3 %select_add_fusion = f32[64,64,128]{2,1,0:T(8,128)} fusion(f32[64,64,128]{2,1,0:T(8,128)} %get-tuple-element.21, f32[64,64,128]{2,1,0:T(8,128)S(1)} %gather_fusion, pred[64]{0:T(512)(128)(4,1)S(1)} %get-tuple-element.6), kind=kLoop, calls=%fused_computation.30 | loop fusion | flops 1048576 | bytes 6291520 | tf_op jit(solution)/shard_map/add | solution.py:89
  (56 shorter events, 16.5 us)
Async XLA Ops:
  6.5 1.2 copy-start
  6.5 168.2 %all-reduce.2.cloned.1.call-start = ((), (), s32[]{:S(2)}) async-start(), calls=%async_computation | async-start | bytes 4194304 | tf_op jit(solution)/shard_map/psum | solution.py:80
  11.1 11.0 %copy-start.4 = (bf16[64,64,128]{2,1,0:T(8,128)(2,1)}, bf16[64,64,128]{2,1,0:T(8,128)(2,1)S(1)}, u32[]{:S(2)}) copy-start(bf16[64,64,128]{2,1,0:T(8,128)(2,1)S(1)} %get-tuple-element.18) | copy-start | bytes 3145732
  11.1 8.8 %copy-start.11 = (s32[64,7]{0,1:T(8,128)S(1)}, s32[64,7]{0,1:T(8,128)}, u32[]{:S(2)}) copy-start(s32[64,7]{0,1:T(8,128)} %param.16) | copy-start | bytes 5380
  11.1 9.1 %copy-start.8 = (bf16[64,64,64]{2,1,0:T(8,128)(2,1)S(1)}, bf16[64,64,64]{2,1,0:T(8,128)(2,1)}, u32[]{:S(2)}) copy-start(bf16[64,64,64]{2,1,0:T(8,128)(2,1)} %param.13) | copy-start | bytes 1572868
  12.2 28.5 %collective-permute-start.1 = (bf16[32,64,128]{2,1,0:T(8,128)(2,1)}, bf16[32,64,128]{2,1,0:T(8,128)(2,1)}, u32[]{:S(2)}, u32[]{:S(2)}) collective-permute-start(bf16[32,64,128]{2,1,0:T(8,128)(2,1)} %get-tuple-element.17), channel_id=1, source_target_pairs={{1,0},{2,1},{3,2},{4,3},{5,4},{6,5},{7,6},{8,7},{9,8},{10,9},{11,1... | collective-permute-start | bytes 1572872 | tf_op jit(solution)/shard_map/ppermute | solution.py:19
  13.6 27.1 %collective-permute-start = (bf16[32,64,128]{2,1,0:T(8,128)(2,1)}, bf16[32,64,128]{2,1,0:T(8,128)(2,1)}, u32[]{:S(2)}, u32[]{:S(2)}) collective-permute-start(bf16[32,64,128]{2,1,0:T(8,128)(2,1)} %get-tuple-element.16), channel_id=1, source_target_pairs={{0,1},{1,2},{2,3},{3,4},{4,5},{5,6},{6,7},{7,8},{8,9},{9,10},{10,1... | collective-permute-start | bytes 1572872 | tf_op jit(solution)/shard_map/ppermute | solution.py:17
  65.9 8.6 %copy-start.5 = (bf16[64,64,128]{2,1,0:T(8,128)(2,1)}, bf16[64,64,128]{2,1,0:T(8,128)(2,1)S(1)}, u32[]{:S(2)}) copy-start(bf16[64,64,128]{2,1,0:T(8,128)(2,1)S(1)} %get-tuple-element.20) | copy-start | bytes 3145732
  65.9 6.8 %copy-start.13 = (s32[64]{0:T(128)S(1)}, s32[64]{0:T(128)}, u32[]{:S(2)}) copy-start(s32[64]{0:T(128)} %param.17) | copy-start | bytes 772
  65.9 6.8 %copy-start.9 = (bf16[64,64,64]{2,1,0:T(8,128)(2,1)S(1)}, bf16[64,64,64]{2,1,0:T(8,128)(2,1)}, u32[]{:S(2)}) copy-start(bf16[64,64,64]{2,1,0:T(8,128)(2,1)} %param.13) | copy-start | bytes 1572868
  65.9 28.0 %collective-permute-start.3 = (bf16[32,64,128]{2,1,0:T(8,128)(2,1)S(1)}, bf16[32,64,128]{2,1,0:T(8,128)(2,1)S(1)}, u32[]{:S(2)}, u32[]{:S(2)}) collective-permute-start(bf16[32,64,128]{2,1,0:T(8,128)(2,1)S(1)} %get-tuple-element.15), channel_id=1, source_target_pairs={{1,0},{2,1},{3,2},{4,3},{5,4},{6,5},{7,6},{8,7},{9,8},{10,9},{11,1... | collective-permute-start | bytes 1572872 | tf_op jit(solution)/shard_map/ppermute | solution.py:19
  67.4 26.7 %collective-permute-start.2 = (bf16[32,64,128]{2,1,0:T(8,128)(2,1)S(1)}, bf16[32,64,128]{2,1,0:T(8,128)(2,1)S(1)}, u32[]{:S(2)}, u32[]{:S(2)}) collective-permute-start(bf16[32,64,128]{2,1,0:T(8,128)(2,1)S(1)} %get-tuple-element.14), channel_id=1, source_target_pairs={{0,1},{1,2},{2,3},{3,4},{4,5},{5,6},{6,7},{7,8},{8,9},{9,10},{10,1... | collective-permute-start | bytes 1572872 | tf_op jit(solution)/shard_map/ppermute | solution.py:17
  121.9 0.7 copy-start.12
  178.8 8.7 %copy-start.2 = (f32[64,128,64]{1,2,0:T(8,128)}, f32[64,128,64]{1,2,0:T(8,128)S(1)}, u32[]{:S(2)}) copy-start(f32[64,128,64]{1,2,0:T(8,128)S(1)} %fusion.23) | copy-start | bytes 6291460
  180.5 15.6 %collective-permute-start.5 = (bf16[32,64,128]{2,1,0:T(8,128)(2,1)}, bf16[32,64,128]{2,1,0:T(8,128)(2,1)}, u32[]{:S(2)}, u32[]{:S(2)}) collective-permute-start(bf16[32,64,128]{2,1,0:T(8,128)(2,1)} %get-tuple-element.13), channel_id=1, source_target_pairs={{1,0},{2,1},{3,2},{4,3},{5,4},{6,5},{7,6},{9,8},{10,9},{11,10},{12... | collective-permute-start | bytes 1572872 | tf_op jit(solution)/shard_map/ppermute | solution.py:19
  182.0 25.2 %collective-permute-start.4 = (bf16[32,64,128]{2,1,0:T(8,128)(2,1)}, bf16[32,64,128]{2,1,0:T(8,128)(2,1)}, u32[]{:S(2)}, u32[]{:S(2)}) collective-permute-start(bf16[32,64,128]{2,1,0:T(8,128)(2,1)} %get-tuple-element.12), channel_id=1, source_target_pairs={{0,1},{1,2},{2,3},{3,4},{4,5},{5,6},{6,7},{8,9},{9,10},{10,11},{11... | collective-permute-start | bytes 1572872 | tf_op jit(solution)/shard_map/ppermute | solution.py:17
  222.0 6.9 %copy-start.6 = (f32[64,64,128]{2,0,1:T(8,128)S(1)}, f32[64,64,128]{2,0,1:T(8,128)}, u32[]{:S(2)}) copy-start(f32[64,64,128]{2,0,1:T(8,128)} %all-reduce.2.cloned.1.call-done) | copy-start | bytes 6291460
  222.0 6.9 %copy-start.7 = (f32[64,128,64]{1,2,0:T(8,128)S(1)}, f32[64,128,64]{1,2,0:T(8,128)}, u32[]{:S(2)}) copy-start(f32[64,128,64]{1,2,0:T(8,128)} %fusion.28) | copy-start | bytes 6291460
  228.9 2.4 copy-start.3
  228.9 2.4 copy-start.10
  236.2 3.3 %copy-start.1 = (bf16[64,64,64]{2,1,0:T(8,128)(2,1)S(1)}, bf16[64,64,64]{2,1,0:T(8,128)(2,1)}, u32[]{:S(2)}) copy-start(bf16[64,64,64]{2,1,0:T(8,128)(2,1)} %param.14) | copy-start | bytes 1572868
Sparse Core Ops, SparseCore 0:
  122.0 52.6 all-reduce.1
where the time goes:
time: 247 us; the launch traced here: 246 us
  waiting for transfers between devices  107 us (43%)
  local copies, waits for them, and re-layouts  47.4 us (19%)
  matrix products  44.8 us (18%)
  starting transfers between devices  21.2 us (9%)
  between operations  13.7 us (6%)
  other arithmetic  12.4 us (5%)
    psum x1, waiting for transfers between devices, on_device(): coarse_rhs = lax.psum(partial_sum, 'grp')  51.9 us
    ppermute x3, waiting for transfers between devices, extended_2(): lax.ppermute(head, axis, [((i + 1) % count, i) for i in range(ends)])  43.5 us
    gather x3, local copies, waits for them, and re-layouts, nearby_product(): nearby = jnp.take(extended, columns - first_row, axis=0)  40 us
    dot_general x7, matrix products, block_product(): jnp.einsum('nab,nbk->nak', blocks, vector.astype(jnp.bfloat16), preferred...  25 us
    ppermute x3, starting transfers between devices, extended_2(): lax.ppermute(tail, axis, [(i, (i + 1) % count) for i in range(ends)])  16.9 us
    dot_general x2, matrix products, nearby_product(): jnp.einsum('njab,njbk->nak', off_blocks, nearby, preferred_element_type=j...  16 us
    ppermute x3, waiting for transfers between devices, extended_2(): lax.ppermute(tail, axis, [(i, (i + 1) % count) for i in range(ends)])  11.4 us
  transfers between devices with their start and end apart: 7, of which 7 were waited for; matrix products, arithmetic and copies ran while one was open for 3% of the time, Pallas kernels for 0%

commit v1 on v0

--- a/solution.py
+++ b/solution.py
@@ -77,7 +77,7 @@
     partial_sum = jnp.einsum(
         "fc,fak->cak", selector, second_residual, precision=lax.Precision.HIGHEST
     )
-    coarse_rhs = lax.psum(partial_sum, "grp")
+    coarse_rhs = jnp.sum(lax.all_gather(partial_sum, "grp"), axis=0)
     coarse_first = damping * block_product(coarse_smoother, coarse_rhs)
     rounded_first = coarse_first.astype(jnp.bfloat16)
     coarse_image = block_product(coarse_diag, rounded_first) + coarse_nearby(

time: 247 us -> 257 us (1.040)
  waiting for transfers between devices: 107 us -> 119 us
  starting transfers between devices: 21.2 us -> 15.6 us
  local copies, waits for them, and re-layouts: 47.4 us -> 50.2 us
    all_gather x0 -> x1, waiting for transfers between devices: none -> 56.6 us  [on_device(): coarse_rhs = jnp.sum(lax.all_gather(partial_sum, 'grp'), axis=0)]
    psum x1 -> x0, waiting for transfers between devices: 51.9 us -> none  [on_device(): coarse_rhs = lax.psum(partial_sum, 'grp')]
    ppermute x3, waiting for transfers between devices: 11.4 us -> 55.6 us  [extended_2(): lax.ppermute(tail, axis, [(i, (i + 1) % count) for i in range(ends)])]
    ppermute x3, waiting for transfers between devices: 43.5 us -> 6.74 us  [extended_2(): lax.ppermute(head, axis, [((i + 1) % count, i) for i in range(ends)])]
    dot_general x2 -> x1, matrix products: 16 us -> 9.17 us  [nearby_product(): jnp.einsum('njab,njbk->nak', off_blocks, nearby, preferred_element_type=j...]
    dot_general x7, matrix products: 25 us -> 31.6 us  [block_product(): jnp.einsum('nab,nbk->nak', blocks, vector.astype(jnp.bfloat16), preferred...]
    ppermute x3, starting transfers between devices: 16.9 us -> 11.5 us  [extended_2(): lax.ppermute(tail, axis, [(i, (i + 1) % count) for i in range(ends)])]
    reduce_sum x0 -> x1, other arithmetic: none -> 4.64 us  [on_device(): coarse_rhs = jnp.sum(lax.all_gather(partial_sum, 'grp'), axis=0)]
  transfers between devices with their start and end apart: 7 -> 7, of which waited for: 7 -> 6; matrix products, arithmetic and copies ran while one was open for 3% -> 3% of each run, Pallas kernels for 0% -> 0%
where the time goes in v1:
time: 257 us; the launch traced here: 256 us
  waiting for transfers between devices  119 us (46%)
  local copies, waits for them, and re-layouts  50.2 us (20%)
  matrix products  44.6 us (17%)
  starting transfers between devices  15.6 us (6%)
  between operations  13.6 us (5%)
  other arithmetic  13.1 us (5%)
    all_gather x1, waiting for transfers between devices, on_device(): coarse_rhs = jnp.sum(lax.all_gather(partial_sum, 'grp'), axis=0)  56.6 us
    ppermute x3, waiting for transfers between devices, extended_2(): lax.ppermute(tail, axis, [(i, (i + 1) % count) for i in range(ends)])  55.6 us
    gather x3, local copies, waits for them, and re-layouts, nearby_product(): nearby = jnp.take(extended, columns - first_row, axis=0)  40.5 us
    dot_general x7, matrix products, block_product(): jnp.einsum('nab,nbk->nak', blocks, vector.astype(jnp.bfloat16), preferred...  31.6 us
    ppermute x3, starting transfers between devices, extended_2(): lax.ppermute(tail, axis, [(i, (i + 1) % count) for i in range(ends)])  11.5 us
    dot_general x1, matrix products, nearby_product(): jnp.einsum('njab,njbk->nak', off_blocks, nearby, preferred_element_type=j...  9.17 us
    ppermute x3, waiting for transfers between devices, extended_2(): lax.ppermute(head, axis, [((i + 1) % count, i) for i in range(ends)])  6.74 us
  transfers between devices with their start and end apart: 7, of which 6 were waited for; matrix products, arithmetic and copies ran while one was open for 3% of the time, Pallas kernels for 0%

profile of v1, /device:TPU:0, one launch (start us, length us, event | category | flops | bytes accessed | tf_op | source)
XLA Modules:
  0.0 256.1 jit_solution(5148456155343866585)
XLA Ops:
  7.8 3.4 %multiply_convert_fusion.1 = (bf16[64,64,128]{2,1,0:T(8,128)(2,1)S(1)}, f32[64,64,128]{2,1,0:T(8,128)}) fusion(bf16[64,64,64]{2,1,0:T(8,128)(2,1)S(1)} %copy-done, f32[64,64,128]{2,1,0:T(8,128)} %param.12), kind=kOutput, calls=%fused_computation.33 | convolution fusion | flops 68681728 | bytes 5767168 | tf_op jit(solution)/shard_map/nab,nbk->nak/dot_general | solution.py:27
  12.2 5.8 %collective-permute-start = (bf16[32,64,128]{2,1,0:T(8,128)(2,1)}, bf16[32,64,128]{2,1,0:T(8,128)(2,1)}, u32[]{:S(2)}, u32[]{:S(2)}) collective-permute-start(bf16[32,64,128]{2,1,0:T(8,128)(2,1)} %get-tuple-element.16), channel_id=1, source_target_pairs={{0,1},{1,2},{2,3},{3,4},{4,5},{5,6},{6,7},{7,8},{8,9},{9,10},{10,1... | collective-permute-start | bytes 1572872 | tf_op jit(solution)/shard_map/ppermute | solution.py:17
  19.6 1.8 fusion.47
  21.5 18.4 %collective-permute-done = bf16[32,64,128]{2,1,0:T(8,128)(2,1)} collective-permute-done((bf16[32,64,128]{2,1,0:T(8,128)(2,1)}, bf16[32,64,128]{2,1,0:T(8,128)(2,1)}, u32[]{:S(2)}, u32[]{:S(2)}) %collective-permute-start) | collective-permute-done | bytes 524320 | tf_op jit(solution)/shard_map/ppermute | solution.py:17
  39.9 4.1 %collective-permute-done.1 = bf16[32,64,128]{2,1,0:T(8,128)(2,1)} collective-permute-done((bf16[32,64,128]{2,1,0:T(8,128)(2,1)}, bf16[32,64,128]{2,1,0:T(8,128)(2,1)}, u32[]{:S(2)}, u32[]{:S(2)}) %collective-permute-start.1) | collective-permute-done | bytes 524320 | tf_op jit(solution)/shard_map/ppermute | solution.py:19
  44.0 1.8 pad_maximum_fusion
  45.7 13.3 %gather_fusion.1 = bf16[448,64,128]{2,1,0:T(8,128)(2,1)} fusion(bf16[128,64,128]{2,1,0:T(8,128)(2,1)S(1)} %pad_maximum_fusion, s32[1024]{0:T(1024)S(1)} %pad_clamp_fusion.2), kind=kCustom, calls=%fused_computation.clone | custom fusion | bytes 14681856 | tf_op jit(solution)/shard_map/jit(_take)/gather | solution.py:33
  59.1 10.1 %fusion.44 = (bf16[64,64,128]{2,1,0:T(8,128)(2,1)S(1)}, f32[64,64,128]{2,1,0:T(8,128)}) fusion(bf16[64,64,64]{2,1,0:T(8,128)(2,1)S(1)} %copy-done, f32[64,64,128]{2,1,0:T(8,128)} %param.12, f32[64,128,64]{1,2,0:T(8,128)} %fusion.47, bf16[64,7,64,64]{3,2,1,0:T(8,128)(2,1)} %param.15, bf16[64,7,64,128]{3,2,1,0:T(8,128)(2,1)} %bitcast.63, ...), kind=kOutput, calls=%fused_computation.60 | convolution fusion | flops 544210944 | bytes 20971968 | tf_op jit(solution)/shard_map/nab,nbk->nak/dot_general | solution.py:27
  69.2 1.6 collective-permute-start.2
  72.4 1.8 fusion.48
  74.2 19.4 %collective-permute-done.2 = bf16[32,64,128]{2,1,0:T(8,128)(2,1)S(1)} collective-permute-done((bf16[32,64,128]{2,1,0:T(8,128)(2,1)S(1)}, bf16[32,64,128]{2,1,0:T(8,128)(2,1)S(1)}, u32[]{:S(2)}, u32[]{:S(2)}) %collective-permute-start.2) | collective-permute-done | bytes 524320 | tf_op jit(solution)/shard_map/ppermute | solution.py:17
  93.6 2.6 %collective-permute-done.3 = bf16[32,64,128]{2,1,0:T(8,128)(2,1)S(1)} collective-permute-done((bf16[32,64,128]{2,1,0:T(8,128)(2,1)S(1)}, bf16[32,64,128]{2,1,0:T(8,128)(2,1)S(1)}, u32[]{:S(2)}, u32[]{:S(2)}) %collective-permute-start.3) | collective-permute-done | bytes 524320 | tf_op jit(solution)/shard_map/ppermute | solution.py:19
  97.7 13.6 %gather_fusion.2 = bf16[448,64,128]{2,1,0:T(8,128)(2,1)} fusion(bf16[128,64,128]{2,1,0:T(8,128)(2,1)S(1)} %pad_maximum_fusion.1, s32[1024]{0:T(1024)S(1)} %pad_clamp_fusion.2), kind=kCustom, calls=%fused_computation.1.clone | custom fusion | bytes 14681856 | tf_op jit(solution)/shard_map/jit(_take)/gather | solution.py:33
  111.3 9.2 %bitcast_subtract_fusion.1 = f32[64,64,128]{2,1,0:T(8,128)S(1)} fusion(f32[64,64,128]{2,1,0:T(8,128)} %param.12, f32[64,128,64]{1,2,0:T(8,128)} %fusion.48, bf16[64,7,64,64]{3,2,1,0:T(8,128)(2,1)} %param.15, bf16[64,7,64,128]{3,2,1,0:T(8,128)(2,1)} %bitcast.65, pred[64,7]{1,0:T(8,128)(4,1)S(1)} %copy.22), kind=kOutput, calls=%fused_computation.22 | convolution fusion | flops 474480640 | bytes 17301952 | tf_op jit(solution)/shard_map/njab,njbk->nak/dot_general | solution.py:34
  120.5 3.9 %fusion.14 = f32[64,64,128]{2,0,1:T(8,128)} fusion(f32[64,64,128]{2,1,0:T(8,128)S(1)} %bitcast_subtract_fusion.1, s32[64]{0:T(128)S(1)} %get-tuple-element.7), kind=kOutput, calls=%fused_computation.28 | convolution fusion | flops 402657280 | bytes 4194560 | tf_op jit(solution)/shard_map/fc,fak->cak/dot_general | solution.py:77
  125.3 56.6 %all-gather.3.cloned.1.call-done = f32[256,64,128]{2,0,1:T(8,128)} async-done(((f32[64,64,128]{2,0,1:T(8,128)}), f32[256,64,128]{2,0,1:T(8,128)}) %all-gather.3.cloned.1.call-update) | async-done | bytes 8388624 | tf_op jit(solution)/shard_map/all_gather | solution.py:80
  181.9 4.6 %reduce_sum.9 = f32[64,64,128]{2,0,1:T(8,128)S(1)} reduce(f32[4,64,64,128]{3,1,0,2:T(8,128)} %bitcast.62, f32[]{:T(128)} %constant.43.clone.1), dimensions={0}, to_apply=%region_0.0 | reduce | flops 1572864 | bytes 10485764 | tf_op jit(solution)/shard_map/reduce_sum | solution.py:80
  191.8 4.1 %collective-permute-start.4 = (bf16[32,64,128]{2,1,0:T(8,128)(2,1)}, bf16[32,64,128]{2,1,0:T(8,128)(2,1)}, u32[]{:S(2)}, u32[]{:S(2)}) collective-permute-start(bf16[32,64,128]{2,1,0:T(8,128)(2,1)} %get-tuple-element.12), channel_id=1, source_target_pairs={{0,1},{1,2},{2,3},{3,4},{4,5},{5,6},{6,7},{8,9},{9,10},{10,11},{11... | collective-permute-start | bytes 1572872 | tf_op jit(solution)/shard_map/ppermute | solution.py:17
  197.4 3.1 %fusion.31 = f32[64,128,64]{1,2,0:T(8,128)} fusion(bf16[64,64,64]{2,1,0:T(8,128)(2,1)} %param.18, f32[64,128,64]{1,2,0:T(8,128)S(1)} %fusion.26), kind=kOutput, calls=%fused_computation.39 | convolution fusion | flops 68157440 | bytes 4718592 | tf_op jit(solution)/shard_map/nab,nbk->nak/dot_general | solution.py:27
  200.5 17.8 %collective-permute-done.4 = bf16[32,64,128]{2,1,0:T(8,128)(2,1)} collective-permute-done((bf16[32,64,128]{2,1,0:T(8,128)(2,1)}, bf16[32,64,128]{2,1,0:T(8,128)(2,1)}, u32[]{:S(2)}, u32[]{:S(2)}) %collective-permute-start.4) | collective-permute-done | bytes 524320 | tf_op jit(solution)/shard_map/ppermute | solution.py:17
  219.8 13.6 %gather_fusion.3 = bf16[448,64,128]{2,1,0:T(8,128)(2,1)} fusion(bf16[128,64,128]{2,1,0:T(8,128)(2,1)S(1)} %pad_maximum_fusion.2, s32[1024]{0:T(1024)S(1)} %pad_clamp_fusion.1), kind=kCustom, calls=%fused_computation.2.clone | custom fusion | bytes 14681856 | tf_op jit(solution)/shard_map/jit(_take)/gather | solution.py:33
  233.4 10.3 %add_bitcast_fusion = f32[64,64,128]{2,1,0:T(8,128)} fusion(f32[64,128,64]{1,2,0:T(8,128)} %copy-done.2, bf16[64,64,64]{2,1,0:T(8,128)(2,1)S(1)} %copy-done.9, f32[64,128,64]{1,2,0:T(8,128)} %fusion.31, f32[64,64,128]{2,0,1:T(8,128)} %copy-done.5, bf16[64,7,64,64]{3,2,1,0:T(8,128)(2,1)} %param.20, bf16[64,7,64,128]{3,2,1,0:T(8,128)(2,1)} %bitcast.64, ...), kind=kOutput, calls=%fused_computation.31 | convolution fusion | flops 543686656 | bytes 19923392 | tf_op jit(solution)/shard_map/nab,nbk->nak/dot_general | solution.py:27
  243.7 2.3 gather_fusion
  246.0 3.3 %select_add_fusion = f32[64,64,128]{2,1,0:T(8,128)} fusion(f32[64,64,128]{2,1,0:T(8,128)} %get-tuple-element.21, f32[64,64,128]{2,1,0:T(8,128)S(1)} %gather_fusion, pred[64]{0:T(512)(128)(4,1)S(1)} %get-tuple-element.6), kind=kLoop, calls=%fused_computation.30 | loop fusion | flops 1048576 | bytes 6291520 | tf_op jit(solution)/shard_map/add | solution.py:89
  (53 shorter events, 16.0 us)
Async XLA Ops:
  6.5 1.2 copy-start
  6.5 175.3 %all-gather.3.cloned.1.call-start = ((), (), s32[]{:S(2)}) async-start(), calls=%async_computation | async-start | bytes 10485760 | tf_op jit(solution)/shard_map/all_gather | solution.py:80
  11.1 10.4 %copy-start.3 = (bf16[64,64,128]{2,1,0:T(8,128)(2,1)}, bf16[64,64,128]{2,1,0:T(8,128)(2,1)S(1)}, u32[]{:S(2)}) copy-start(bf16[64,64,128]{2,1,0:T(8,128)(2,1)S(1)} %get-tuple-element.18) | copy-start | bytes 3145732
  11.1 8.1 %copy-start.10 = (s32[64,7]{0,1:T(8,128)S(1)}, s32[64,7]{0,1:T(8,128)}, u32[]{:S(2)}) copy-start(s32[64,7]{0,1:T(8,128)} %param.16) | copy-start | bytes 5380
  11.1 8.5 %copy-start.6 = (bf16[64,64,64]{2,1,0:T(8,128)(2,1)S(1)}, bf16[64,64,64]{2,1,0:T(8,128)(2,1)}, u32[]{:S(2)}) copy-start(bf16[64,64,64]{2,1,0:T(8,128)(2,1)} %param.13) | copy-start | bytes 1572868
  12.2 27.7 %collective-permute-start = (bf16[32,64,128]{2,1,0:T(8,128)(2,1)}, bf16[32,64,128]{2,1,0:T(8,128)(2,1)}, u32[]{:S(2)}, u32[]{:S(2)}) collective-permute-start(bf16[32,64,128]{2,1,0:T(8,128)(2,1)} %get-tuple-element.16), channel_id=1, source_target_pairs={{0,1},{1,2},{2,3},{3,4},{4,5},{5,6},{6,7},{7,8},{8,9},{9,10},{10,1... | collective-permute-start | bytes 1572872 | tf_op jit(solution)/shard_map/ppermute | solution.py:17
  17.9 26.0 %collective-permute-start.1 = (bf16[32,64,128]{2,1,0:T(8,128)(2,1)}, bf16[32,64,128]{2,1,0:T(8,128)(2,1)}, u32[]{:S(2)}, u32[]{:S(2)}) collective-permute-start(bf16[32,64,128]{2,1,0:T(8,128)(2,1)} %get-tuple-element.17), channel_id=1, source_target_pairs={{1,0},{2,1},{3,2},{4,3},{5,4},{6,5},{7,6},{8,7},{9,8},{10,9},{11,1... | collective-permute-start | bytes 1572872 | tf_op jit(solution)/shard_map/ppermute | solution.py:19
  69.2 5.1 %copy-start.4 = (bf16[64,64,128]{2,1,0:T(8,128)(2,1)}, bf16[64,64,128]{2,1,0:T(8,128)(2,1)S(1)}, u32[]{:S(2)}) copy-start(bf16[64,64,128]{2,1,0:T(8,128)(2,1)S(1)} %get-tuple-element.20) | copy-start | bytes 3145732
  69.2 3.2 %copy-start.12 = (s32[64]{0:T(128)S(1)}, s32[64]{0:T(128)}, u32[]{:S(2)}) copy-start(s32[64]{0:T(128)} %param.17) | copy-start | bytes 772
  69.2 3.2 %copy-start.7 = (bf16[64,64,64]{2,1,0:T(8,128)(2,1)S(1)}, bf16[64,64,64]{2,1,0:T(8,128)(2,1)}, u32[]{:S(2)}) copy-start(bf16[64,64,64]{2,1,0:T(8,128)(2,1)} %param.13) | copy-start | bytes 1572868
  69.2 24.4 %collective-permute-start.2 = (bf16[32,64,128]{2,1,0:T(8,128)(2,1)S(1)}, bf16[32,64,128]{2,1,0:T(8,128)(2,1)S(1)}, u32[]{:S(2)}, u32[]{:S(2)}) collective-permute-start(bf16[32,64,128]{2,1,0:T(8,128)(2,1)S(1)} %get-tuple-element.14), channel_id=1, source_target_pairs={{0,1},{1,2},{2,3},{3,4},{4,5},{5,6},{6,7},{7,8},{8,9},{9,10},{10,1... | collective-permute-start | bytes 1572872 | tf_op jit(solution)/shard_map/ppermute | solution.py:17
  70.9 25.4 %collective-permute-start.3 = (bf16[32,64,128]{2,1,0:T(8,128)(2,1)S(1)}, bf16[32,64,128]{2,1,0:T(8,128)(2,1)S(1)}, u32[]{:S(2)}, u32[]{:S(2)}) collective-permute-start(bf16[32,64,128]{2,1,0:T(8,128)(2,1)S(1)} %get-tuple-element.15), channel_id=1, source_target_pairs={{1,0},{2,1},{3,2},{4,3},{5,4},{6,5},{7,6},{8,7},{9,8},{10,9},{11,1... | collective-permute-start | bytes 1572872 | tf_op jit(solution)/shard_map/ppermute | solution.py:19
  124.3 0.7 copy-start.11
  186.5 1.3 copy-start.5
  187.8 1.2 copy-start.8
  190.2 7.2 %copy-start.2 = (f32[64,128,64]{1,2,0:T(8,128)}, f32[64,128,64]{1,2,0:T(8,128)S(1)}, u32[]{:S(2)}) copy-start(f32[64,128,64]{1,2,0:T(8,128)S(1)} %fusion.26) | copy-start | bytes 6291460
  191.8 26.5 %collective-permute-start.4 = (bf16[32,64,128]{2,1,0:T(8,128)(2,1)}, bf16[32,64,128]{2,1,0:T(8,128)(2,1)}, u32[]{:S(2)}, u32[]{:S(2)}) collective-permute-start(bf16[32,64,128]{2,1,0:T(8,128)(2,1)} %get-tuple-element.12), channel_id=1, source_target_pairs={{0,1},{1,2},{2,3},{3,4},{4,5},{5,6},{6,7},{8,9},{9,10},{10,11},{11... | collective-permute-start | bytes 1572872 | tf_op jit(solution)/shard_map/ppermute | solution.py:17
  196.0 22.4 %collective-permute-start.5 = (bf16[32,64,128]{2,1,0:T(8,128)(2,1)}, bf16[32,64,128]{2,1,0:T(8,128)(2,1)}, u32[]{:S(2)}, u32[]{:S(2)}) collective-permute-start(bf16[32,64,128]{2,1,0:T(8,128)(2,1)} %get-tuple-element.13), channel_id=1, source_target_pairs={{1,0},{2,1},{3,2},{4,3},{5,4},{6,5},{7,6},{9,8},{10,9},{11,10},{12... | collective-permute-start | bytes 1572872 | tf_op jit(solution)/shard_map/ppermute | solution.py:19
  219.7 13.6 %copy-start.9 = (bf16[64,64,64]{2,1,0:T(8,128)(2,1)S(1)}, bf16[64,64,64]{2,1,0:T(8,128)(2,1)}, u32[]{:S(2)}) copy-start(bf16[64,64,64]{2,1,0:T(8,128)(2,1)} %param.19) | copy-start | bytes 1572868
  246.0 3.3 %copy-start.1 = (bf16[64,64,64]{2,1,0:T(8,128)(2,1)S(1)}, bf16[64,64,64]{2,1,0:T(8,128)(2,1)}, u32[]{:S(2)}) copy-start(bf16[64,64,64]{2,1,0:T(8,128)(2,1)} %param.14) | copy-start | bytes 1572868
Sparse Core Ops, SparseCore 0:
  124.5 57.3 all-gather.2
